TPU v7x, 32 devices: a whole 2x2x4 slice. The times are simulated.
32 devices in a mesh: prow: 4 (over y, core), pcol: 8 (over z, x).
Axes of the slice: x: 2, y: 2, z: 4, core: 2. Of those that a mesh axis runs over, the one named last changes fastest.
Arguments:
- matrix: bfloat16 [2, 8, 4, 256, 2, 8, 256], P(None, None, 'prow', None, None, 'pcol'), may hold values from -6 to 6
Outputs:
- image: float32 [2, 8, 4, 256, 2, 8, 256], P(None, None, 'prow', None, None, 'pcol')
All inputs are finite; a program needn't handle non-finite values.
Results may differ from a plain program's by a relative error of at most 0.0003.
Values sent between devices are 32-bit elements; how exact they have to be, the bound alone decides.
A program may use at most 64 MiB of HBM per device.

v0:
```python
import jax
import jax.numpy as jnp
from jax import lax
from jax.sharding import PartitionSpec as P

HIGH = lax.Precision.HIGHEST


def prefix(value, axis, combine, identity):
    length, here = (lax.axis_size(axis), lax.axis_index(axis))
    everything = lax.all_gather(value, axis)
    start = jnp.broadcast_to(jnp.asarray(identity, value.dtype), value.shape)

    def lap(k, before):
        reached = k < here
        new = combine(before, everything[k])
        return jnp.where(reached, new, before)

    return lax.fori_loop(0, length, lap, start)


def add_terms(earlier, later):
    return earlier + later


def shards(matrix):
    batch = matrix.shape[0]
    rows_here = matrix.shape[1]
    tile_len = matrix.shape[3]
    cols_here = matrix.shape[4]
    prow_count = lax.axis_size("prow")
    pcol_count = lax.axis_size("pcol")
    prow_index = lax.axis_index("prow")
    pcol_index = lax.axis_index("pcol")
    local = matrix.astype(jnp.float32).reshape(batch, rows_here, tile_len, cols_here, tile_len)
    first_idx = lax.broadcasted_iota(jnp.int32, (tile_len, tile_len), 0)
    second_idx = lax.broadcasted_iota(jnp.int32, (tile_len, tile_len), 1)
    upper = (first_idx <= second_idx).astype(jnp.float32)
    lower = (second_idx <= first_idx).astype(jnp.float32)
    rowscan = jnp.einsum("nrick,kj->nricj", local, upper, precision=HIGH)
    row_sums = rowscan[:, :, :, :, tile_len - 1]
    gathered = lax.all_gather(row_sums, "pcol", axis=3, tiled=True)
    source = jnp.arange(pcol_count * cols_here, dtype=jnp.int32)
    source_glob = source % cols_here * pcol_count + source // cols_here
    target_glob = jnp.arange(cols_here, dtype=jnp.int32) * pcol_count + pcol_index
    earlier_mask = (source_glob[:, None] < target_glob[None, :]).astype(jnp.float32)
    row_carry = jnp.einsum("nrig,gc->nric", gathered, earlier_mask, precision=HIGH)
    rowscan = rowscan + row_carry[:, :, :, :, None]
    colscan = jnp.einsum("ik,nrkcj->nricj", lower, rowscan, precision=HIGH)
    col_sums = colscan[:, :, tile_len - 1, :, :]
    before = prefix(col_sums, "prow", add_terms, jnp.zeros_like(col_sums))
    whole = lax.psum(col_sums, "prow")
    strict = (jnp.arange(rows_here)[:, None] < jnp.arange(rows_here)[None, :]).astype(jnp.float32)
    col_carry = before + jnp.einsum("nscj,sr->nrcj", whole, strict, precision=HIGH)
    colscan = colscan + col_carry[:, :, None, :, :]
    row_glob = (
        jnp.arange(rows_here, dtype=jnp.int32)[:, None] * prow_count + prow_index
    ) * tile_len + jnp.arange(tile_len, dtype=jnp.int32)[None, :]
    col_glob = (
        jnp.arange(cols_here, dtype=jnp.int32)[:, None] * pcol_count + pcol_index
    ) * tile_len + jnp.arange(tile_len, dtype=jnp.int32)[None, :]
    row_factor = 1.0 / jnp.sqrt(row_glob.astype(jnp.float32) + 1.0)
    col_factor = 1.0 / jnp.sqrt(col_glob.astype(jnp.float32) + 1.0)
    scaled = colscan * (row_factor[None, :, :, None, None] * col_factor[None, None, None, :, :])
    return scaled.reshape(batch, rows_here, 1, tile_len, cols_here, 1, tile_len)


def solution(mesh):
    return jax.shard_map(
        shards,
        mesh=mesh,
        in_specs=(P(None, None, "prow", None, None, "pcol", None),),
        out_specs=P(None, None, "prow", None, None, "pcol", None),
        check_vma=False,
    )
```

profile of v0, /device:TPU:0, one launch (start us, length us, event | category | flops | bytes accessed | tf_op | source)
XLA Modules:
  0.0 76.3 jit_solution(13902189001919219110)
XLA Ops:
  0.0 3.5 %fusion.8 = f32[2,8,256,2,256]{2,4,3,1,0:T(8,128)S(1)} fusion(bf16[2,8,256,2,256]{4,3,2,1,0:T(2,128)(2,1)} %bitcast.44), kind=kOutput, calls=%fused_computation.10 | convolution fusion | flops 1073807360 | bytes 12582912 | tf_op jit(solution)/shard_map/nrick,kj->nricj/dot_general | solution.py:40
  3.5 28.3 %all-gather = f32[2,8,256,16,1]{2,4,3,1,0:T(1,128)S(1)} all-gather(f32[2,8,256,2,1]{2,4,3,1,0:T(1,128)S(1)} %slice.8), channel_id=2, replica_groups=mesh['prow'=4,'pcol'=8] {'pcol'}, dimensions={3}, use_global_device_ids=true | all-gather | bytes 294912 | tf_op jit(solution)/shard_map/all_gather | solution.py:42
  31.9 0.3 fusion.12
  32.2 4.9 %fusion.5 = f32[2,8,256,2,256]{4,2,3,1,0:T(8,128)S(1)} fusion(f32[2,8,256,2,256]{2,4,3,1,0:T(8,128)S(1)} %fusion.8, f32[2,8,256,2]{2,3,1,0:T(2,128)S(1)} %fusion.12), kind=kOutput, calls=%fused_computation.9 | convolution fusion | flops 6444613632 | bytes 16809984 | tf_op jit(solution)/shard_map/ik,nrkcj->nricj/dot_general | solution.py:49
  37.2 0.0 copy-start
  37.2 3.4 %copy-done = f32[2,8,256,2,256]{4,2,3,1,0:T(8,128)} copy-done((f32[2,8,256,2,256]{4,2,3,1,0:T(8,128)}, f32[2,8,256,2,256]{4,2,3,1,0:T(8,128)S(1)}, u32[]{:S(2)}) %copy-start) | copy-done | bytes 8388632
  40.6 5.4 %all-gather.1 = f32[8,8,1,2,256]{4,1,3,2,0:T(8,128)S(1)} all-gather(f32[2,8,1,2,256]{4,1,3,2,0:T(8,128)S(1)} %copy.10), channel_id=3, replica_groups=mesh['prow'=4,'pcol'=8] {'prow'}, dimensions={0}, use_global_device_ids=true | all-gather | bytes 163840 | tf_op jit(solution)/shard_map/all_gather | solution.py:11
  46.0 0.3 while.14
  46.3 11.6 %psum.7 = f32[2,8,2,256]{3,2,1,0:T(2,128)S(1)} all-reduce(f32[2,8,2,256]{3,2,1,0:T(2,128)S(1)} %bitcast.46), channel_id=1, replica_groups=mesh['prow'=4,'pcol'=8] {'prow'}, use_global_device_ids=true, to_apply=%region_2.3 | all-reduce | flops 8192 | bytes 65536 | tf_op jit(solution)/shard_map/psum | solution.py:52
  58.0 0.1 fusion.11
  58.1 0.1 add_rsqrt_fusion
  58.2 0.1 add_rsqrt_fusion.1
  58.3 2.3 %broadcast_multiply_fusion = f32[8,256,2,256]{3,1,2,0:T(8,128)} fusion(f32[2,256]{1,0:T(2,128)S(1)} %add_rsqrt_fusion.1, f32[8,256]{1,0:T(8,128)S(1)} %add_rsqrt_fusion), kind=kLoop, calls=%fused_computation.11 | loop fusion | flops 1048576 | bytes 4204544 | tf_op jit(solution)/shard_map/mul | solution.py:64
  60.6 5.8 %multiply_bitcast_fusion = f32[2,8,1,256,2,1,256]{6,3,4,1,0,5,2:T(8,128)S(1)} fusion(f32[2,8,256,2,256]{4,2,3,1,0:T(8,128)} %copy-done, f32[8,256,2,256]{3,1,2,0:T(8,128)} %broadcast_multiply_fusion, f32[2,8,2,256]{3,2,1,0:T(2,128)S(1)} %copy.14), kind=kLoop, calls=%fused_computation.3 | loop fusion | flops 4194304 | bytes 21004288 | tf_op jit(solution)/shard_map/reshape | solution.py:65
  66.4 9.9 %copy.15 = f32[2,8,1,256,2,1,256]{6,5,4,3,2,1,0:T(1,128)} copy(f32[2,8,1,256,2,1,256]{6,3,4,1,0,5,2:T(8,128)S(1)} %multiply_bitcast_fusion) | data formatting | bytes 16777216 | tf_op jit(solution)/shard_map/reshape | solution.py:65
  (18 shorter events, 0.3 us)
Async XLA Ops:
  37.2 3.4 %copy-start = (f32[2,8,256,2,256]{4,2,3,1,0:T(8,128)}, f32[2,8,256,2,256]{4,2,3,1,0:T(8,128)S(1)}, u32[]{:S(2)}) copy-start(f32[2,8,256,2,256]{4,2,3,1,0:T(8,128)S(1)} %fusion.5) | copy-start | bytes 25165828
where the time goes:
time: 76.5 us; the launch traced here: 76.3 us
  blocking collectives  45.4 us (59%)
  local copies, waits for them, and re-layouts  13.4 us (18%)
  matrix products  8.87 us (12%)
  other arithmetic  8.4 us (11%)
    all_gather x1, blocking collectives, shards(): gathered = lax.all_gather(row_sums, 'pcol', axis=3, tiled=True)  28.3 us
    psum x1, blocking collectives, shards(): whole = lax.psum(col_sums, 'prow')  11.6 us
    reshape x1, local copies, waits for them, and re-layouts, shards(): return scaled.reshape(batch, rows_here, 1, tile_len, cols_here, 1, tile_len)  9.91 us
    reshape x1, other arithmetic, shards(): return scaled.reshape(batch, rows_here, 1, tile_len, cols_here, 1, tile_len)  5.81 us
    all_gather x1, blocking collectives, prefix(): everything = lax.all_gather(value, axis)  5.42 us
    dot_general x1, matrix products, shards(): colscan = jnp.einsum('ik,nrkcj->nricj', lower, rowscan, precision=HIGH)  4.93 us
    dot_general x1, matrix products, shards(): rowscan = jnp.einsum('nrick,kj->nricj', local, upper, precision=HIGH)  3.48 us
    unnamed x3, local copies, waits for them, and re-layouts  3.41 us

commit v1 on v0

--- a/solution.py
+++ b/solution.py
@@ -39,12 +39,42 @@
     lower = (second_idx <= first_idx).astype(jnp.float32)
     rowscan = jnp.einsum("nrick,kj->nricj", local, upper, precision=HIGH)
     row_sums = rowscan[:, :, :, :, tile_len - 1]
-    gathered = lax.all_gather(row_sums, "pcol", axis=3, tiled=True)
     source = jnp.arange(pcol_count * cols_here, dtype=jnp.int32)
     source_glob = source % cols_here * pcol_count + source // cols_here
     target_glob = jnp.arange(cols_here, dtype=jnp.int32) * pcol_count + pcol_index
     earlier_mask = (source_glob[:, None] < target_glob[None, :]).astype(jnp.float32)
-    row_carry = jnp.einsum("nrig,gc->nric", gathered, earlier_mask, precision=HIGH)
+    size, index, span = (lax.axis_size("pcol"), lax.axis_index("pcol"), row_sums.shape[3])
+    right = [(i, (i + 1) % size) for i in range(size)]
+    behind = [(i, (i - 1) % size) for i in range(size)]
+    middle = size // 2
+    from_left = from_right = row_sums
+    so_far = jnp.einsum(
+        "nrig,gc->nric",
+        row_sums,
+        lax.dynamic_slice_in_dim(earlier_mask, index * span, row_sums.shape[3], axis=0),
+        precision=HIGH,
+    )
+    for hop in range(1, middle + 1):
+        from_left = lax.ppermute(from_left, "pcol", right)
+        if hop < size - middle:
+            from_right = lax.ppermute(from_right, "pcol", behind)
+            so_far = so_far + jnp.einsum(
+                "nrig,gc->nric",
+                from_right,
+                lax.dynamic_slice_in_dim(
+                    earlier_mask, (index + hop) % size * span, from_right.shape[3], axis=0
+                ),
+                precision=HIGH,
+            )
+        so_far = so_far + jnp.einsum(
+            "nrig,gc->nric",
+            from_left,
+            lax.dynamic_slice_in_dim(
+                earlier_mask, (index - hop) % size * span, from_left.shape[3], axis=0
+            ),
+            precision=HIGH,
+        )
+    row_carry = so_far
     rowscan = rowscan + row_carry[:, :, :, :, None]
     colscan = jnp.einsum("ik,nrkcj->nricj", lower, rowscan, precision=HIGH)
     col_sums = colscan[:, :, tile_len - 1, :, :]

time: 76.5 us -> 83.9 us (1.097)
  blocking collectives: 45.4 us -> 17 us
  starting transfers between devices: 0 us -> 15.6 us
  waiting for transfers between devices: 0 us -> 12.3 us
  matrix products: 8.87 us -> 13 us
  local copies, waits for them, and re-layouts: 13.4 us -> 16.8 us
    all_gather x1 -> x0, blocking collectives: 28.3 us -> none  [shards(): gathered = lax.all_gather(row_sums, 'pcol', axis=3, tiled=True)]
    ppermute x0 -> x7, starting transfers between devices: none -> 15.6 us  [the longest x3 15.5 us: shards(): from_right = lax.ppermute(from_right, 'pcol', behind)]
    ppermute x0 -> x7, waiting for transfers between devices: none -> 12.3 us  [the longest x4 12.3 us: shards(): from_left = lax.ppermute(from_left, 'pcol', right)]
    unnamed x3 -> x6, local copies, waits for them, and re-layouts: 3.41 us -> 6.82 us
    dot_general x1, matrix products: 4.93 us -> 7.27 us  [shards(): colscan = jnp.einsum('ik,nrkcj->nricj', lower, rowscan, precision=HIGH)]
    dot_general x1 -> x8, matrix products: 0.32 us -> 2.09 us  [the longest x4 1.04 us: shards(): jnp.einsum('nrig,gc->nric', from_left, lax.dynamic_slice_in_dim(earlier_m...]
  transfers between devices with their start and end apart: 0 -> 7, of which waited for: 0 -> 4; matrix products, arithmetic and copies ran while one was open for 0% -> 5% of each run, Pallas kernels for 0% -> 0%
where the time goes in v1:
time: 83.9 us; the launch traced here: 83.7 us
  blocking collectives  17 us (20%)
  local copies, waits for them, and re-layouts  16.8 us (20%)
  starting transfers between devices  15.6 us (19%)
  matrix products  13 us (15%)
  waiting for transfers between devices  12.3 us (15%)
  other arithmetic  8.5 us (10%)
    ppermute x3, starting transfers between devices, shards(): from_right = lax.ppermute(from_right, 'pcol', behind)  15.5 us
    ppermute x4, waiting for transfers between devices, shards(): from_left = lax.ppermute(from_left, 'pcol', right)  12.3 us
    psum x1, blocking collectives, shards(): whole = lax.psum(col_sums, 'prow')  11.6 us
    reshape x1, local copies, waits for them, and re-layouts, shards(): return scaled.reshape(batch, rows_here, 1, tile_len, cols_here, 1, tile_len)  9.91 us
    dot_general x1, matrix products, shards(): colscan = jnp.einsum('ik,nrkcj->nricj', lower, rowscan, precision=HIGH)  7.27 us
    unnamed x6, local copies, waits for them, and re-layouts  6.82 us
    reshape x1, other arithmetic, shards(): return scaled.reshape(batch, rows_here, 1, tile_len, cols_here, 1, tile_len)  5.82 us
    all_gather x1, blocking collectives, prefix(): everything = lax.all_gather(value, axis)  5.42 us
  transfers between devices with their start and end apart: 7, of which 4 were waited for; matrix products, arithmetic and copies ran while one was open for 5% of the time, Pallas kernels for 0%

profile of v1, /device:TPU:0, one launch (start us, length us, event | category | flops | bytes accessed | tf_op | source)
XLA Modules:
  0.0 83.7 jit_solution(17544186583274987937)
XLA Ops:
  0.0 3.5 %fusion.8 = f32[2,8,256,2,256]{2,4,3,1,0:T(8,128)S(1)} fusion(bf16[2,8,256,2,256]{4,3,2,1,0:T(2,128)(2,1)} %bitcast.87), kind=kOutput, calls=%fused_computation.10 | convolution fusion | flops 1073807360 | bytes 12582912 | tf_op jit(solution)/shard_map/nrick,kj->nricj/dot_general | solution.py:40
  3.5 0.0 copy-start.1
  3.5 3.4 %copy-done.1 = f32[2,8,256,2,256]{2,4,3,1,0:T(8,128)} copy-done((f32[2,8,256,2,256]{2,4,3,1,0:T(8,128)}, f32[2,8,256,2,256]{2,4,3,1,0:T(8,128)S(1)}, u32[]{:S(2)}) %copy-start.1) | copy-done | bytes 8388632
  6.9 6.1 %collective-permute-start = (f32[2,8,256,2]{2,3,1,0:T(2,128)S(1)}, f32[2,8,256,2]{2,3,1,0:T(2,128)S(1)}, u32[]{:S(2)}, u32[]{:S(2)}) collective-permute-start(f32[2,8,256,2]{2,3,1,0:T(2,128)S(1)} %bitcast.89), channel_id=1, source_target_pairs={{0,7},{1,0},{2,1},{3,2},{4,3},{5,4},{6,5},{7,6},{8,15},{9,8},{10,9... | collective-permute-start | bytes 98312 | tf_op jit(solution)/shard_map/ppermute | solution.py:60
  13.0 0.0 collective-permute-start.1
  13.0 0.1 add_rsqrt_fusion.1
  13.1 0.1 add_rsqrt_fusion
  13.2 0.1 broadcast_compare_fusion
  13.3 2.3 %broadcast_multiply_fusion = f32[8,256,2,256]{3,1,2,0:T(8,128)} fusion(f32[2,256]{1,0:T(2,128)S(1)} %add_rsqrt_fusion.1, f32[8,256]{1,0:T(8,128)S(1)} %add_rsqrt_fusion), kind=kLoop, calls=%fused_computation.11 | loop fusion | flops 1048576 | bytes 4204544 | tf_op jit(solution)/shard_map/mul | solution.py:94
  15.6 0.3 fusion.22
  16.0 3.6 %collective-permute-done.1 = f32[2,8,256,2]{2,3,1,0:T(2,128)S(1)} collective-permute-done((f32[2,8,256,2]{2,3,1,0:T(2,128)S(1)}, f32[2,8,256,2]{2,3,1,0:T(2,128)S(1)}, u32[]{:S(2)}, u32[]{:S(2)}) %collective-permute-start.1) | collective-permute-done | bytes 32800 | tf_op jit(solution)/shard_map/ppermute | solution.py:58
  19.6 0.0 collective-permute-start.3
  19.6 0.0 collective-permute-done
  19.6 4.7 %collective-permute-start.2 = (f32[2,8,256,2]{2,3,1,0:T(2,128)S(1)}, f32[2,8,256,2]{2,3,1,0:T(2,128)S(1)}, u32[]{:S(2)}, u32[]{:S(2)}) collective-permute-start(f32[2,8,256,2]{2,3,1,0:T(2,128)S(1)} %collective-permute-done), channel_id=1, source_target_pairs={{0,7},{1,0},{2,1},{3,2},{4,3},{5,4},{6,5},{7,6},{8,15},{9,8},{10,9... | collective-permute-start | bytes 98312 | tf_op jit(solution)/shard_map/ppermute | solution.py:60
  24.3 0.3 convolution_add_fusion.4
  24.6 0.3 convolution_add_fusion.3
  24.9 1.3 %collective-permute-done.3 = f32[2,8,256,2]{2,3,1,0:T(2,128)S(1)} collective-permute-done((f32[2,8,256,2]{2,3,1,0:T(2,128)S(1)}, f32[2,8,256,2]{2,3,1,0:T(2,128)S(1)}, u32[]{:S(2)}, u32[]{:S(2)}) %collective-permute-start.3) | collective-permute-done | bytes 32800 | tf_op jit(solution)/shard_map/ppermute | solution.py:58
  26.2 0.0 collective-permute-start.5
  26.2 0.3 fusion.31
  26.5 0.0 collective-permute-done.2
  26.5 4.8 %collective-permute-start.4 = (f32[2,8,256,2]{2,3,1,0:T(2,128)S(1)}, f32[2,8,256,2]{2,3,1,0:T(2,128)S(1)}, u32[]{:S(2)}, u32[]{:S(2)}) collective-permute-start(f32[2,8,256,2]{2,3,1,0:T(2,128)S(1)} %collective-permute-done.2), channel_id=1, source_target_pairs={{0,7},{1,0},{2,1},{3,2},{4,3},{5,4},{6,5},{7,6},{8,15},{9,8},{10,9... | collective-permute-start | bytes 98312 | tf_op jit(solution)/shard_map/ppermute | solution.py:60
  31.3 0.3 fusion.13
  31.6 1.3 %collective-permute-done.5 = f32[2,8,256,2]{2,3,1,0:T(2,128)S(1)} collective-permute-done((f32[2,8,256,2]{2,3,1,0:T(2,128)S(1)}, f32[2,8,256,2]{2,3,1,0:T(2,128)S(1)}, u32[]{:S(2)}, u32[]{:S(2)}) %collective-permute-start.5) | collective-permute-done | bytes 32800 | tf_op jit(solution)/shard_map/ppermute | solution.py:58
  32.8 0.0 collective-permute-start.6
  32.8 0.3 fusion.36
  33.1 0.0 collective-permute-done.4
  33.1 0.3 fusion.12
  33.4 6.1 %collective-permute-done.6 = f32[2,8,256,2]{2,3,1,0:T(2,128)S(1)} collective-permute-done((f32[2,8,256,2]{2,3,1,0:T(2,128)S(1)}, f32[2,8,256,2]{2,3,1,0:T(2,128)S(1)}, u32[]{:S(2)}, u32[]{:S(2)}) %collective-permute-start.6) | collective-permute-done | bytes 32800 | tf_op jit(solution)/shard_map/ppermute | solution.py:58
  39.5 0.3 convolution_add_fusion
  39.7 7.3 %fusion.5 = f32[2,8,256,2,256]{4,2,3,1,0:T(8,128)S(1)} fusion(f32[2,8,256,2,256]{2,4,3,1,0:T(8,128)} %copy-done.1, f32[2,8,256,2]{2,3,1,0:T(2,128)S(1)} %convolution_add_fusion), kind=kOutput, calls=%fused_computation.9 | convolution fusion | flops 6444613632 | bytes 16809984 | tf_op jit(solution)/shard_map/ik,nrkcj->nricj/dot_general | solution.py:79
  47.0 0.0 copy-start
  47.0 3.4 %copy-done = f32[2,8,256,2,256]{4,2,3,1,0:T(8,128)} copy-done((f32[2,8,256,2,256]{4,2,3,1,0:T(8,128)}, f32[2,8,256,2,256]{4,2,3,1,0:T(8,128)S(1)}, u32[]{:S(2)}) %copy-start) | copy-done | bytes 8388632
  50.5 5.4 %all-gather = f32[8,8,1,2,256]{4,1,3,2,0:T(8,128)S(1)} all-gather(f32[2,8,1,2,256]{4,1,3,2,0:T(8,128)S(1)} %copy.10), channel_id=2, replica_groups=mesh['prow'=4,'pcol'=8] {'prow'}, dimensions={0}, use_global_device_ids=true | all-gather | bytes 163840 | tf_op jit(solution)/shard_map/all_gather | solution.py:11
  55.9 0.3 while.14
  56.2 11.6 %psum.7 = f32[2,8,2,256]{3,2,1,0:T(2,128)S(1)} all-reduce(f32[2,8,2,256]{3,2,1,0:T(2,128)S(1)} %bitcast.92), channel_id=1, replica_groups=mesh['prow'=4,'pcol'=8] {'prow'}, use_global_device_ids=true, to_apply=%region_2.3 | all-reduce | flops 8192 | bytes 65536 | tf_op jit(solution)/shard_map/psum | solution.py:82
  67.8 0.1 fusion.11
  68.0 5.8 %multiply_bitcast_fusion = f32[2,8,1,256,2,1,256]{6,3,4,1,0,5,2:T(8,128)S(1)} fusion(f32[2,8,256,2,256]{4,2,3,1,0:T(8,128)} %copy-done, f32[8,256,2,256]{3,1,2,0:T(8,128)} %broadcast_multiply_fusion, f32[2,8,2,256]{3,2,1,0:T(2,128)S(1)} %copy.14), kind=kLoop, calls=%fused_computation.3 | loop fusion | flops 4194304 | bytes 21004288 | tf_op jit(solution)/shard_map/reshape | solution.py:95
  73.8 9.9 %copy.15 = f32[2,8,1,256,2,1,256]{6,5,4,3,2,1,0:T(1,128)} copy(f32[2,8,1,256,2,1,256]{6,3,4,1,0,5,2:T(8,128)S(1)} %multiply_bitcast_fusion) | data formatting | bytes 16777216 | tf_op jit(solution)/shard_map/reshape | solution.py:95
  (19 shorter events, 0.3 us)
Async XLA Ops:
  3.5 3.4 %copy-start.1 = (f32[2,8,256,2,256]{2,4,3,1,0:T(8,128)}, f32[2,8,256,2,256]{2,4,3,1,0:T(8,128)S(1)}, u32[]{:S(2)}) copy-start(f32[2,8,256,2,256]{2,4,3,1,0:T(8,128)S(1)} %fusion.8) | copy-start | bytes 25165828
  6.9 12.7 %collective-permute-start = (f32[2,8,256,2]{2,3,1,0:T(2,128)S(1)}, f32[2,8,256,2]{2,3,1,0:T(2,128)S(1)}, u32[]{:S(2)}, u32[]{:S(2)}) collective-permute-start(f32[2,8,256,2]{2,3,1,0:T(2,128)S(1)} %bitcast.89), channel_id=1, source_target_pairs={{0,7},{1,0},{2,1},{3,2},{4,3},{5,4},{6,5},{7,6},{8,15},{9,8},{10,9... | collective-permute-start | bytes 98312 | tf_op jit(solution)/shard_map/ppermute | solution.py:60
  13.0 6.6 %collective-permute-start.1 = (f32[2,8,256,2]{2,3,1,0:T(2,128)S(1)}, f32[2,8,256,2]{2,3,1,0:T(2,128)S(1)}, u32[]{:S(2)}, u32[]{:S(2)}) collective-permute-start(f32[2,8,256,2]{2,3,1,0:T(2,128)S(1)} %bitcast.90), channel_id=1, source_target_pairs={{0,1},{1,2},{2,3},{3,4},{4,5},{5,6},{6,7},{7,0},{8,9},{9,10},{10,1... | collective-permute-start | bytes 98312 | tf_op jit(solution)/shard_map/ppermute | solution.py:58
  19.6 6.6 %collective-permute-start.3 = (f32[2,8,256,2]{2,3,1,0:T(2,128)S(1)}, f32[2,8,256,2]{2,3,1,0:T(2,128)S(1)}, u32[]{:S(2)}, u32[]{:S(2)}) collective-permute-start(f32[2,8,256,2]{2,3,1,0:T(2,128)S(1)} %collective-permute-done.1), channel_id=1, source_target_pairs={{0,1},{1,2},{2,3},{3,4},{4,5},{5,6},{6,7},{7,0},{8,9},{9,10},{10,1... | collective-permute-start | bytes 98312 | tf_op jit(solution)/shard_map/ppermute | solution.py:58
  19.6 6.9 %collective-permute-start.2 = (f32[2,8,256,2]{2,3,1,0:T(2,128)S(1)}, f32[2,8,256,2]{2,3,1,0:T(2,128)S(1)}, u32[]{:S(2)}, u32[]{:S(2)}) collective-permute-start(f32[2,8,256,2]{2,3,1,0:T(2,128)S(1)} %collective-permute-done), channel_id=1, source_target_pairs={{0,7},{1,0},{2,1},{3,2},{4,3},{5,4},{6,5},{7,6},{8,15},{9,8},{10,9... | collective-permute-start | bytes 98312 | tf_op jit(solution)/shard_map/ppermute | solution.py:60
  26.2 6.6 %collective-permute-start.5 = (f32[2,8,256,2]{2,3,1,0:T(2,128)S(1)}, f32[2,8,256,2]{2,3,1,0:T(2,128)S(1)}, u32[]{:S(2)}, u32[]{:S(2)}) collective-permute-start(f32[2,8,256,2]{2,3,1,0:T(2,128)S(1)} %collective-permute-done.3), channel_id=1, source_target_pairs={{0,1},{1,2},{2,3},{3,4},{4,5},{5,6},{6,7},{7,0},{8,9},{9,10},{10,1... | collective-permute-start | bytes 98312 | tf_op jit(solution)/shard_map/ppermute | solution.py:58
  26.5 6.6 %collective-permute-start.4 = (f32[2,8,256,2]{2,3,1,0:T(2,128)S(1)}, f32[2,8,256,2]{2,3,1,0:T(2,128)S(1)}, u32[]{:S(2)}, u32[]{:S(2)}) collective-permute-start(f32[2,8,256,2]{2,3,1,0:T(2,128)S(1)} %collective-permute-done.2), channel_id=1, source_target_pairs={{0,7},{1,0},{2,1},{3,2},{4,3},{5,4},{6,5},{7,6},{8,15},{9,8},{10,9... | collective-permute-start | bytes 98312 | tf_op jit(solution)/shard_map/ppermute | solution.py:60
  32.8 6.6 %collective-permute-start.6 = (f32[2,8,256,2]{2,3,1,0:T(2,128)S(1)}, f32[2,8,256,2]{2,3,1,0:T(2,128)S(1)}, u32[]{:S(2)}, u32[]{:S(2)}) collective-permute-start(f32[2,8,256,2]{2,3,1,0:T(2,128)S(1)} %collective-permute-done.5), channel_id=1, source_target_pairs={{0,1},{1,2},{2,3},{3,4},{4,5},{5,6},{6,7},{7,0},{8,9},{9,10},{10,1... | collective-permute-start | bytes 98312 | tf_op jit(solution)/shard_map/ppermute | solution.py:58
  47.0 3.4 %copy-start = (f32[2,8,256,2,256]{4,2,3,1,0:T(8,128)}, f32[2,8,256,2,256]{4,2,3,1,0:T(8,128)S(1)}, u32[]{:S(2)}) copy-start(f32[2,8,256,2,256]{4,2,3,1,0:T(8,128)S(1)} %fusion.5) | copy-start | bytes 25165828
